TPU v7x, 32 devices: a whole 2x2x4 slice. The times are simulated.
32 devices in a mesh: node: 4 (over x, core), local: 8 (over z, y).
Axes of the slice: x: 2, y: 2, z: 4, core: 2. Of those that a mesh axis runs over, the one named last changes fastest.
Arguments:
- tokens: bfloat16 [2048, 7168], P(('node', 'local')), may hold values from -6 to 6
- routes: int32 [2048, 2], P(('node', 'local')), may hold values from 0 to 7, as said below
- scores: float32 [2048, 2], P(('node', 'local')), may hold values from 0.1 to 1
- gate_proj: bfloat16 [32, 7168, 512], P(('node', 'local')), may hold values from -0.0625 to 0.0625
- up_proj: bfloat16 [32, 7168, 512], P(('node', 'local')), may hold values from -0.0625 to 0.0625
- down_proj: bfloat16 [32, 512, 7168], P(('node', 'local')), may hold values from -0.125 to 0.125
Outputs:
- combined: bfloat16 [2048, 7168], P(('node', 'local'))
Inputs may be any that keep to these rules, and one draw needn't show every extreme that they name: `routes`: each row names 2 different experts. The rows of one device name each expert at most 20 times, and in every draw one expert is named by exactly 20 rows of every device.
All inputs are finite; a program needn't handle non-finite values.
Results may differ from a plain program's by a relative error of at most 0.0085.
Values may be sent and summed in bfloat16 or wider, within the bound.
A program may use at most 192 MiB of HBM per device.

v0:
```python
import jax
import jax.numpy as jnp
from jax import lax
from jax.sharding import PartitionSpec as P

SHARDS = 4


SCALE = 2.827


def expert_block(block_rows, w_gate, w_up, w_down):
    block_shape = block_rows.shape
    flat_rows = block_rows.reshape(-1, block_shape[-1])
    gate_act = jnp.dot(flat_rows, w_gate, preferred_element_type=jnp.float32)
    up_act = jnp.dot(flat_rows, w_up, preferred_element_type=jnp.float32)
    hidden = (jax.nn.silu(gate_act) * up_act).astype(jnp.bfloat16)
    partial_value = jnp.dot(hidden, w_down, preferred_element_type=jnp.float32).astype(jnp.bfloat16)
    return partial_value.reshape(block_shape[:-1] + (w_down.shape[1],))


def per_device(tokens, routes, scores, gate_proj, up_proj, down_proj):
    node_count = lax.axis_size("node")
    local_count = lax.axis_size("local")
    token_count, model_width = tokens.shape
    top_count = routes.shape[1]
    node_experts = local_count // SHARDS
    experts = node_count * node_experts
    per_expert = max(
        2, token_count * top_count // experts + token_count * top_count // (4 * experts)
    )
    w_gate = gate_proj[0]
    w_up = up_proj[0]
    w_down = down_proj[0]
    weights = (SCALE * scores / jnp.sum(scores, axis=1, keepdims=True)).astype(jnp.bfloat16)
    labels = jnp.arange(experts, dtype=jnp.int32)
    matches = routes[:, :, None] == labels[None, None, :]
    dense_weight = jnp.sum(jnp.where(matches, weights.astype(jnp.float32)[:, :, None], 0.0), axis=1)
    routed = dense_weight > 0
    position = jnp.cumsum(routed.astype(jnp.int32), axis=0) - 1
    slot_ids = jnp.arange(per_expert, dtype=jnp.int32)
    slot_pick = (routed[None] & (position[None] == slot_ids[:, None, None])).astype(jnp.bfloat16)
    bucket = jnp.einsum(
        "cte,td->ecd", slot_pick, tokens, preferred_element_type=jnp.float32
    ).astype(jnp.bfloat16)
    outgoing = jnp.broadcast_to(
        bucket[:, None], (experts, SHARDS, per_expert, model_width)
    ).reshape(experts * SHARDS, per_expert, model_width)
    results = expert_block(
        lax.all_to_all(outgoing, ("node", "local"), split_axis=0, concat_axis=0, tiled=True),
        w_gate,
        w_up,
        w_down,
    )
    returned = lax.all_to_all(results, ("node", "local"), split_axis=0, concat_axis=0, tiled=True)
    summed = jnp.sum(
        returned.reshape(experts, SHARDS, per_expert, model_width).astype(jnp.float32), axis=1
    )
    gathered = summed[labels[None, :], jnp.clip(position, 0, per_expert - 1)]
    combined = jnp.sum(gathered * dense_weight[:, :, None], axis=1)
    return combined.astype(jnp.bfloat16)


def solution(mesh):
    return jax.shard_map(
        per_device,
        mesh=mesh,
        in_specs=(
            P(("node", "local"), None),
            P(("node", "local"), None),
            P(("node", "local"), None),
            P(("node", "local"), None, None),
            P(("node", "local"), None, None),
            P(("node", "local"), None, None),
        ),
        out_specs=P(("node", "local"), None),
        check_vma=False,
    )
```

profile of v0, /device:TPU:0, one launch (start us, length us, event | category | flops | bytes accessed | tf_op | source)
XLA Modules:
  0.0 622.5 jit_solution(18273634157123973583)
XLA Ops:
  0.0 0.8 reduce_sum.36
  0.8 0.7 fusion.22
  1.5 0.7 select_reduce_fusion
  2.2 0.1 copy.23
  2.2 0.1 reduce_window_sum.11
  2.4 0.1 copy.24
  2.4 0.7 fusion.1
  3.2 2.9 copy.25
  6.1 7.3 %broadcast_in_dim.18 = bf16[8,4,20,7168]{3,2,1,0:T(8,128)(2,1)} broadcast(bf16[8,20,7168]{2,1,0:T(8,128)(2,1)} %copy.25), dimensions={0,2,3} | broadcast | bytes 11468800 | tf_op jit(solution)/shard_map/broadcast_in_dim | solution.py:46
  13.4 248.4 %all_to_all.10 = bf16[32,20,7168]{2,1,0:T(8,128)(2,1)} all-to-all(bf16[32,20,7168]{2,1,0:T(8,128)(2,1)} %bitcast.33), channel_id=1, replica_groups=mesh['node'=4,'local'=8] {'node','local'}, dimensions={0} | all-to-all | bytes 18350080 | tf_op jit(solution)/shard_map/all_to_all | solution.py:50
  261.8 13.4 %reshape.51 = bf16[640,7168]{1,0:T(8,128)(2,1)} reshape(bf16[32,20,7168]{2,1,0:T(8,128)(2,1)} %all_to_all.10) | data formatting | bytes 18350080 | tf_op jit(solution)/shard_map/reshape | solution.py:14
  275.1 9.7 %fusion.5 = f32[640,512]{1,0:T(8,128)S(1)} fusion(bf16[640,7168]{1,0:T(8,128)(2,1)} %reshape.51, bf16[1,7168,512]{2,1,0:T(8,128)(2,1)} %param.9), kind=kOutput, calls=%fused_computation.10 | convolution fusion | flops 4697620480 | bytes 17825792 | tf_op jit(solution)/shard_map/dot_general | solution.py:15
  284.8 0.0 slice-start.1
  284.9 8.2 %fusion.10 = bf16[640,512]{1,0:T(8,128)(2,1)S(1)} fusion(bf16[640,7168]{1,0:T(8,128)(2,1)S(1)} %copy-done.2, bf16[1,7168,512]{2,1,0:T(8,128)(2,1)} %param.10, f32[640,512]{1,0:T(8,128)S(1)} %fusion.5), kind=kOutput, calls=%fused_computation.13 | convolution fusion | flops 4699586560 | bytes 18481152 | tf_op jit(solution)/shard_map/dot_general | solution.py:16
  293.1 7.3 %convolution_convert_fusion = bf16[640,7168]{1,0:T(8,128)(2,1)} fusion(bf16[640,512]{1,0:T(8,128)(2,1)S(1)} %fusion.10, bf16[1,512,7168]{2,1,0:T(8,128)(2,1)S(1)} %bitcast.35), kind=kOutput, calls=%fused_computation.4 | convolution fusion | flops 4702208000 | bytes 17170432 | tf_op jit(solution)/shard_map/dot_general | solution.py:18
  300.4 13.2 %reshape.52 = bf16[32,20,7168]{2,1,0:T(8,128)(2,1)} reshape(bf16[640,7168]{1,0:T(8,128)(2,1)} %convolution_convert_fusion) | data formatting | bytes 18350080 | tf_op jit(solution)/shard_map/reshape | solution.py:19
  313.7 3.9 all-to-all-start.1
  317.6 0.1 copy.27
  317.7 0.1 reshape.54
  317.8 247.4 %all-to-all-done.1 = bf16[32,20,7168]{2,1,0:T(8,128)(2,1)} async-done(((bf16[32,20,7168]{2,1,0:T(8,128)(2,1)}), bf16[32,20,7168]{2,1,0:T(8,128)(2,1)}, u32[]{:S(2)}, u32[]{:S(2)}) %all-to-all-start.1) | async-done | bytes 9175072 | tf_op jit(solution)/shard_map/all_to_all | solution.py:55
  565.1 9.2 %convert_reduce_fusion = f32[8,20,7168]{2,1,0:T(8,128)} fusion(bf16[32,20,7168]{2,1,0:T(8,128)(2,1)} %all-to-all-done.1), kind=kLoop, calls=%fused_computation.1 | loop fusion | flops 8028160 | bytes 13762560 | tf_op jit(solution)/shard_map/reduce_sum | solution.py:56
  574.4 7.3 %copy.26 = f32[8,20,7168]{2,0,1:T(8,128)} copy(f32[8,20,7168]{2,1,0:T(8,128)} %convert_reduce_fusion) | data formatting | bytes 9175040 | tf_op jit(solution)/shard_map/reduce_sum | solution.py:56
  581.6 29.5 %gather_fusion = f32[512,7168]{1,0:T(8,128)} fusion(f32[8,20,7168]{2,0,1:T(8,128)} %copy.26, s32[512]{0:T(512)S(1)} %reshape.54), kind=kCustom, calls=%fused_computation | custom fusion | bytes 29364224 | tf_op jit(solution)/shard_map/gather | solution.py:59
  611.2 11.3 %fusion = bf16[64,7168]{1,0:T(8,128)(2,1)} fusion(f32[512,7168]{1,0:T(8,128)} %gather_fusion, f32[64,8]{1,0:T(8,128)S(1)} %copy.27), kind=kLoop, calls=%fused_computation.3 | loop fusion | flops 6881280 | bytes 15599616 | tf_op jit(solution)/shard_map/reduce_sum | solution.py:60
  (13 shorter events, 0.1 us)
Async XLA Ops:
  0.0 2.4 copy-start
  275.1 9.7 %copy-start.2 = (bf16[640,7168]{1,0:T(8,128)(2,1)S(1)}, bf16[640,7168]{1,0:T(8,128)(2,1)}, u32[]{:S(2)}) copy-start(bf16[640,7168]{1,0:T(8,128)(2,1)} %reshape.51) | copy-start | bytes 27525124
  275.1 18.0 %slice-start = ((s8[7340032]{0:T(1024)(128)(4,1)}), s8[4194304]{0:T(1024)(128)(4,1)S(1)}, s32[]{:S(2)}) async-start(s8[7340032]{0:T(1024)(128)(4,1)} %bitcast.34), calls=%async_computation.2 | async-start | bytes 8388608
  284.8 8.3 %slice-start.1 = ((s8[7340032]{0:T(1024)(128)(4,1)}), s8[3145728]{0:T(1024)(128)(4,1)S(1)}, s32[]{:S(2)}) async-start(s8[7340032]{0:T(1024)(128)(4,1)} %bitcast.34), calls=%async_computation.3 | async-start | bytes 6291456
  313.7 251.5 %all-to-all-start.1 = ((bf16[32,20,7168]{2,1,0:T(8,128)(2,1)}), bf16[32,20,7168]{2,1,0:T(8,128)(2,1)}, u32[]{:S(2)}, u32[]{:S(2)}) async-start(bf16[32,20,7168]{2,1,0:T(8,128)(2,1)} %reshape.52), calls=%async_computation.1 | async-start | bytes 22020096 | tf_op jit(solution)/shard_map/all_to_all | solution.py:55
  581.6 40.9 %copy-start.1 = (bf16[64,7168]{1,0:T(8,128)(2,1)S(1)}, bf16[64,7168]{1,0:T(8,128)(2,1)}, u32[]{:S(2)}) copy-start(bf16[64,7168]{1,0:T(8,128)(2,1)} %param.6) | copy-start | bytes 2752516
where the time goes:
time: 624 us; the launch traced here: 623 us
  blocking collectives  248 us (40%)
  waiting for transfers between devices  247 us (40%)
  local copies, waits for them, and re-layouts  74 us (12%)
  matrix products  26 us (4%)
  other arithmetic  22.8 us (4%)
    all_to_all x1, blocking collectives, per_device(): lax.all_to_all(outgoing, ('node', 'local'), split_axis=0, concat_axis=0,...  248 us
    all_to_all x1, waiting for transfers between devices, per_device(): lax.all_to_all(results, ('node', 'local'), split_axis=0, concat_axis=0, t...  247 us
    gather x1, local copies, waits for them, and re-layouts, per_device(): gathered = summed[labels[None, :], jnp.clip(position, 0, per_expert - 1)]  29.5 us
    reshape x1, local copies, waits for them, and re-layouts, expert_block(): flat_rows = block_rows.reshape(-1, block_shape[-1])  13.4 us
    reshape x1, local copies, waits for them, and re-layouts, expert_block(): return partial_value.reshape(block_shape[:-1] + (w_down.shape[1],))  13.2 us
  transfers between devices with their start and end apart: 1, of which 1 were waited for; matrix products, arithmetic and copies ran while one was open for 0% of the time, Pallas kernels for 0%

commit v1 on v0

v1 whole, which is shorter than its diff:
```python
import functools

import jax
import jax.numpy as jnp
from jax import lax
from jax.experimental import pallas as pl
from jax.experimental.pallas import tpu as pltpu
from jax.sharding import PartitionSpec as P

SHARDS = 4
SCALE = 2.827
MESH = pl.DeviceIdType.MESH


def place(groups):
    node = lax.axis_index("node")
    local = lax.axis_index("local")
    mine = node * groups + local // SHARDS
    block = local % SHARDS
    near = block + 1 - 2 * (block % 2)
    far = (block + 2) % SHARDS
    corner = (near + 2) % SHARDS

    def device(expert, which):
        return (expert // groups, (expert % groups) * SHARDS + which)

    return mine, block, near, far, corner, device


def greet(mine, block, near, far, device, experts):
    barrier = pltpu.get_barrier_semaphore()
    targets = [device((mine + r) % experts, block) for r in range(1, experts)]
    targets += [device(mine, near), device(mine, far)]
    for target in targets:
        pl.semaphore_signal(barrier, inc=1, device_id=target, device_id_type=MESH)
    pl.semaphore_wait(barrier, len(targets))


def over_far(r):
    return r % 4 == 0


def dispatch_kernel(experts, groups, bucket, out, own_sem, a_send, a_recv, b_send, b_recv, c_send, c_recv):
    mine, block, near, far, corner, device = place(groups)
    greet(mine, block, near, far, device, experts)

    def remote(src, dst, send, recv, target):
        return pltpu.make_async_remote_copy(
            src_ref=src, dst_ref=dst, send_sem=send, recv_sem=recv, device_id=target, device_id_type=MESH
        )

    spread = {}
    for r in range(1, experts):
        peer = (mine + r) % experts
        spread[r] = remote(bucket.at[peer], out.at[block, mine], a_send.at[r], a_recv.at[r], device(peer, block))
        spread[r].start()
    own = pltpu.make_async_copy(bucket.at[mine], out.at[block, mine], own_sem)
    own.start()

    order = list(range(experts))
    to_near, to_far, relay = {}, {}, {}

    def forward(r):
        source = (mine + experts - r) % experts
        if over_far(r):
            to_near[r].wait_recv()
            relay[r] = remote(out.at[near, source], out.at[near, source], c_send.at[r], c_recv.at[r], device(mine, far))
        else:
            to_far[r].wait_recv()
            relay[r] = remote(out.at[far, source], out.at[far, source], c_send.at[r], c_recv.at[r], device(mine, near))
        relay[r].start()

    for step, r in enumerate(order):
        source = (mine + experts - r) % experts
        if r == 0:
            src = bucket.at[mine]
        else:
            spread[r].wait_recv()
            src = out.at[block, source]
        to_near[r] = remote(src, out.at[block, source], b_send.at[0, r], b_recv.at[0, r], device(mine, near))
        to_far[r] = remote(src, out.at[block, source], b_send.at[1, r], b_recv.at[1, r], device(mine, far))
        to_near[r].start()
        to_far[r].start()
        if step >= 2:
            forward(order[step - 2])
    for r in order[-2:]:
        forward(r)
    for r in order:
        if over_far(r):
            to_far[r].wait_recv()
        else:
            to_near[r].wait_recv()
        relay[r].wait_recv()
    for r in order:
        if r:
            spread[r].wait_send()
        to_near[r].wait_send()
        to_far[r].wait_send()
        relay[r].wait_send()
    own.wait()


def combine_kernel(experts, groups, part, ret, held, total, back, a_send, a_recv, b_send, b_recv, c_send, c_recv):
    mine, block, near, far, corner, device = place(groups)
    greet(mine, block, near, far, device, experts)

    def remote(src, dst, send, recv, target):
        return pltpu.make_async_remote_copy(
            src_ref=src, dst_ref=dst, send_sem=send, recv_sem=recv, device_id=target, device_id_type=MESH
        )

    def wide(ref):
        return ref[...].astype(jnp.float32)

    order = list(range(1, experts)) + [0]
    relay, to_near, to_far, home = {}, {}, {}, {}
    for r in order:
        source = (mine + experts - r) % experts
        target = far if over_far(r) else near
        relay[r] = remote(part.at[corner, source], held.at[2, r], c_send.at[r], c_recv.at[r], device(mine, target))
        relay[r].start()
        if over_far(r):
            to_far[r] = remote(part.at[far, source], held.at[1, r], b_send.at[1, r], b_recv.at[1, r], device(mine, far))
            to_far[r].start()
        else:
            to_near[r] = remote(part.at[near, source], held.at[0, r], b_send.at[0, r], b_recv.at[0, r], device(mine, near))
            to_near[r].start()

    def send_home(r):
        source = (mine + experts - r) % experts
        to_near[r].wait_recv()
        to_far[r].wait_recv()
        value = (wide(part.at[block, source]) + wide(held.at[0, r]) + wide(held.at[1, r])).astype(jnp.bfloat16)
        if r == 0:
            ret[mine] = value
        else:
            back[r] = value
            home[r] = remote(back.at[r], ret.at[mine], a_send.at[r], a_recv.at[r], device(source, block))
            home[r].start()

    for step, r in enumerate(order):
        source = (mine + experts - r) % experts
        relay[r].wait_recv()
        if over_far(r):
            total[r] = (wide(part.at[near, source]) + wide(held.at[2, r])).astype(jnp.bfloat16)
            to_near[r] = remote(total.at[r], held.at[0, r], b_send.at[0, r], b_recv.at[0, r], device(mine, near))
            to_near[r].start()
        else:
            total[r] = (wide(part.at[far, source]) + wide(held.at[2, r])).astype(jnp.bfloat16)
            to_far[r] = remote(total.at[r], held.at[1, r], b_send.at[1, r], b_recv.at[1, r], device(mine, far))
            to_far[r].start()
        if step >= 2:
            send_home(order[step - 2])
    for r in order[-2:]:
        send_home(r)
    for r in order:
        if r:
            home[r].wait()
        relay[r].wait_send()
        to_near[r].wait_send()
        to_far[r].wait_send()


def sems(experts):
    dma = pltpu.SemaphoreType.DMA
    return [dma((experts,)), dma((experts,)), dma((2, experts)), dma((2, experts)), dma((experts,)), dma((experts,))]


def dispatch(bucket, groups):
    experts, cap, width = bucket.shape
    return pl.pallas_call(
        functools.partial(dispatch_kernel, experts, groups),
        out_shape=jax.ShapeDtypeStruct((SHARDS, experts, cap, width), bucket.dtype),
        in_specs=[pl.BlockSpec(memory_space=pltpu.VMEM)],
        out_specs=pl.BlockSpec(memory_space=pl.ANY),
        scratch_shapes=[pltpu.SemaphoreType.DMA] + sems(experts),
        compiler_params=pltpu.CompilerParams(collective_id=0, has_side_effects=True),
        name="dispatch",
    )(bucket)


def combine(part, groups):
    shards, experts, cap, width = part.shape
    block = (experts, cap, width)
    return pl.pallas_call(
        functools.partial(combine_kernel, experts, groups),
        out_shape=jax.ShapeDtypeStruct(block, part.dtype),
        in_specs=[pl.BlockSpec(memory_space=pltpu.VMEM)],
        out_specs=pl.BlockSpec(memory_space=pltpu.VMEM),
        scratch_shapes=[
            pltpu.VMEM((3,) + block, part.dtype),
            pltpu.VMEM(block, part.dtype),
            pltpu.VMEM(block, part.dtype),
        ]
        + sems(experts),
        compiler_params=pltpu.CompilerParams(
            collective_id=1, has_side_effects=True, vmem_limit_bytes=60 * 2**20
        ),
        name="combine",
    )(part)


def expert_block(rows, w_gate, w_up, w_down):
    gate_act = jnp.dot(rows, w_gate, preferred_element_type=jnp.float32)
    up_act = jnp.dot(rows, w_up, preferred_element_type=jnp.float32)
    hidden = (jax.nn.silu(gate_act) * up_act).astype(jnp.bfloat16)
    return jnp.dot(hidden, w_down, preferred_element_type=jnp.float32).astype(jnp.bfloat16)


def per_device(tokens, routes, scores, gate_proj, up_proj, down_proj):
    node_count = lax.axis_size("node")
    local_count = lax.axis_size("local")
    token_count, model_width = tokens.shape
    top_count = routes.shape[1]
    groups = local_count // SHARDS
    experts = node_count * groups
    per_expert = max(
        2, token_count * top_count // experts + token_count * top_count // (4 * experts)
    )
    cap = (per_expert + 7) // 8 * 8
    weights = (SCALE * scores / jnp.sum(scores, axis=1, keepdims=True)).astype(jnp.bfloat16)
    labels = jnp.arange(experts, dtype=jnp.int32)
    matches = routes[:, :, None] == labels[None, None, :]
    routed = jnp.any(matches, axis=1)
    dense_weight = jnp.sum(jnp.where(matches, weights.astype(jnp.float32)[:, :, None], 0.0), axis=1)
    position = jnp.cumsum(routed.astype(jnp.int32), axis=0) - 1
    slot_ids = jnp.arange(cap, dtype=jnp.int32)
    pick = routed.T[:, None, :] & (position.T[:, None, :] == slot_ids[None, :, None])
    slot_pick = pick.astype(jnp.bfloat16).reshape(experts * cap, token_count)
    slot_weight = jnp.where(pick, dense_weight.T[:, None, :], 0.0).astype(jnp.bfloat16)
    slot_weight = slot_weight.reshape(experts * cap, token_count)
    bucket = jnp.dot(slot_pick, tokens, preferred_element_type=jnp.float32).astype(jnp.bfloat16)
    gathered = dispatch(bucket.reshape(experts, cap, model_width), groups)
    rows = gathered.reshape(SHARDS * experts * cap, model_width)
    part = expert_block(rows, gate_proj[0], up_proj[0], down_proj[0])
    returned = combine(part.reshape(SHARDS, experts, cap, model_width), groups)
    combined = lax.dot_general(
        slot_weight,
        returned.reshape(experts * cap, model_width),
        (((0,), (0,)), ((), ())),
        preferred_element_type=jnp.float32,
    )
    return combined.astype(jnp.bfloat16)


def solution(mesh):
    return jax.shard_map(
        per_device,
        mesh=mesh,
        in_specs=(
            P(("node", "local"), None),
            P(("node", "local"), None),
            P(("node", "local"), None),
            P(("node", "local"), None, None),
            P(("node", "local"), None, None),
            P(("node", "local"), None, None),
        ),
        out_specs=P(("node", "local"), None),
        check_vma=False,
    )
```

time: 624 us -> 320 us (0.51)
  Pallas kernels: 0 us -> 282 us
  blocking collectives: 248 us -> 0 us
  waiting for transfers between devices: 247 us -> 0 us
  local copies, waits for them, and re-layouts: 74 us -> 0.25 us
  other arithmetic: 22.8 us -> 1.02 us
  matrix products: 26 us -> 36.4 us
    pallas_call x0 -> x2, Pallas kernels: none -> 282 us  [the longest x1 145 us: dispatch(): pl.pallas_call(functools.partial(dispatch_kernel, experts, groups), out_s...]
    all_to_all x1 -> x0, blocking collectives: 248 us -> none  [per_device(): lax.all_to_all(outgoing, ('node', 'local'), split_axis=0, concat_axis=0,...]
    all_to_all x1 -> x0, waiting for transfers between devices: 247 us -> none  [per_device(): lax.all_to_all(results, ('node', 'local'), split_axis=0, concat_axis=0, t...]
    gather x1 -> x0, local copies, waits for them, and re-layouts: 29.5 us -> none  [per_device(): gathered = summed[labels[None, :], jnp.clip(position, 0, per_expert - 1)]]
    reshape x2 -> x0, local copies, waits for them, and re-layouts: 26.6 us -> none  [the longest x1 13.4 us: expert_block(): flat_rows = block_rows.reshape(-1, block_shape[-1])]
    reduce_sum x2 -> x0, other arithmetic: 20.6 us -> none  [the longest x1 11.3 us: per_device(): combined = jnp.sum(gathered * dense_weight[:, :, None], axis=1)]
    reduce_sum x2 -> x0, local copies, waits for them, and re-layouts: 7.36 us -> none  [the longest x1 7.27 us: per_device(): jnp.sum(returned.reshape(experts, SHARDS, per_expert, model_width).astype...]
    broadcast_in_dim x1 -> x0, local copies, waits for them, and re-layouts: 7.3 us -> none  [per_device(): jnp.broadcast_to(bucket[:, None], (experts, SHARDS, per_expert, model_wid...]
  transfers between devices with their start and end apart: 1 -> 0, of which waited for: 1 -> 0; matrix products, arithmetic and copies ran while one was open for 0% -> 0% of each run, Pallas kernels for 0% -> 0%
where the time goes in v1:
time: 320 us
  Pallas kernels  282 us (88%)
  matrix products  36.4 us (11%)
    pallas_call x1, Pallas kernels, dispatch(): pl.pallas_call(functools.partial(dispatch_kernel, experts, groups), out_s...  145 us
    pallas_call x1, Pallas kernels, combine(): pl.pallas_call(functools.partial(combine_kernel, experts, groups), out_sh...  137 us
    dot_general x1, matrix products, expert_block(): jnp.dot(hidden, w_down, preferred_element_type=jnp.float32)  11.6 us
    dot_general x1, matrix products, expert_block(): gate_act = jnp.dot(rows, w_gate, preferred_element_type=jnp.float32)  10.9 us
    dot_general x1, matrix products, expert_block(): up_act = jnp.dot(rows, w_up, preferred_element_type=jnp.float32)  8.1 us

profile of v1, /device:TPU:0, one launch (start us, length us, event | category | flops | bytes accessed | tf_op | source)
XLA Modules:
  0.0 319.9 jit_solution(12196865247999835317)
XLA Ops:
  0.0 0.0 copy-start
  0.0 0.8 fusion.18
  0.8 0.1 copy.11
  0.9 0.1 reduce_window_sum.11
  1.0 0.1 copy.12
  1.0 0.1 eq.45
  1.1 0.1 fusion.13
  1.2 0.0 copy-done
  1.2 2.5 convolution_convert_fusion.1
  3.7 145.0 %dispatch.1 = bf16[4,8,24,7168]{3,2,1,0:T(8,128)(2,1)} custom-call(bf16[8,24,7168]{2,1,0:T(8,128)(2,1)} %bitcast.36), custom_call_target="tpu_custom_call" | custom-call | tf_op jit(solution)/shard_map/dispatch/pallas_call | solution.py:171
  148.7 0.0 copy-start.1
  148.8 10.9 %fusion.4 = f32[768,512]{1,0:T(8,128)S(1)} fusion(bf16[768,7168]{1,0:T(8,128)(2,1)} %bitcast.37, bf16[1,7168,512]{2,1,0:T(8,128)(2,1)} %param.9), kind=kOutput, calls=%fused_computation.7 | convolution fusion | flops 5637144576 | bytes 19922944 | tf_op jit(solution)/shard_map/dot_general | solution.py:204
  159.6 0.0 copy-done.1
  159.7 8.1 %fusion.9 = bf16[768,512]{1,0:T(8,128)(2,1)S(1)} fusion(bf16[768,7168]{1,0:T(8,128)(2,1)S(1)} %bitcast.38, bf16[1,7168,512]{2,1,0:T(8,128)(2,1)} %param.10, f32[768,512]{1,0:T(8,128)S(1)} %fusion.4), kind=kOutput, calls=%fused_computation.10 | convolution fusion | flops 5639503872 | bytes 20709376 | tf_op jit(solution)/shard_map/dot_general | solution.py:205
  167.8 11.6 %convolution_convert_fusion = bf16[768,7168]{1,0:T(8,128)(2,1)} fusion(bf16[768,512]{1,0:T(8,128)(2,1)S(1)} %fusion.9, bf16[1,512,7168]{2,1,0:T(8,128)(2,1)} %param.11), kind=kOutput, calls=%fused_computation | convolution fusion | flops 5642649600 | bytes 19136512 | tf_op jit(solution)/shard_map/dot_general | solution.py:207
  179.4 0.0 copy-start.2
  179.4 0.0 copy-start.3
  179.4 137.1 %combine.1 = bf16[8,24,7168]{2,1,0:T(8,128)(2,1)} custom-call(bf16[4,8,24,7168]{3,2,1,0:T(8,128)(2,1)} %bitcast.39), custom_call_target="tpu_custom_call" | custom-call | tf_op jit(solution)/shard_map/combine/pallas_call | solution.py:185
  316.5 0.0 copy-done.2
  316.5 0.0 copy-done.3
  316.6 3.4 %fusion = bf16[64,7168]{1,0:T(8,128)(2,1)} fusion(bf16[8,24,7168]{2,1,0:T(8,128)(2,1)} %combine.1, bf16[8,64]{1,0:T(8,128)(2,1)S(1)} %bitcast.42, s32[8,64]{1,0:T(8,128)S(1)} %copy.12, pred[8,64]{1,0:T(8,128)(4,1)S(1)} %bitcast.41), kind=kOutput, calls=%fused_computation.3 | convolution fusion | flops 176656384 | bytes 3673600 | tf_op jit(solution)/shard_map/dot_general | solution.py:237
  (6 shorter events, 0.1 us)
Async XLA Ops:
  0.0 1.2 copy-start
  148.7 10.9 %copy-start.1 = (bf16[4,8,24,7168]{3,2,1,0:T(8,128)(2,1)S(1)}, bf16[4,8,24,7168]{3,2,1,0:T(8,128)(2,1)}, u32[]{:S(2)}) copy-start(bf16[4,8,24,7168]{3,2,1,0:T(8,128)(2,1)} %dispatch.1) | copy-start | bytes 33030148
  179.4 137.1 %copy-start.2 = (f32[64,2]{0,1:T(2,128)S(1)}, f32[64,2]{0,1:T(2,128)}, u32[]{:S(2)}) copy-start(f32[64,2]{0,1:T(2,128)} %param.8) | copy-start | bytes 1540
  179.4 137.2 %copy-start.3 = (s32[64,2]{0,1:T(2,128)S(1)}, s32[64,2]{0,1:T(2,128)}, u32[]{:S(2)}) copy-start(s32[64,2]{0,1:T(2,128)} %param.7) | copy-start | bytes 1540

commit v2 on v1

v2 whole, which is shorter than its diff:
```python
import functools

import jax
import jax.numpy as jnp
from jax import lax
from jax.experimental import pallas as pl
from jax.experimental.pallas import tpu as pltpu
from jax.sharding import PartitionSpec as P

SHARDS = 4
SCALE = 2.827
FOLD = 4
MESH = pl.DeviceIdType.MESH


def place(groups):
    node = lax.axis_index("node")
    local = lax.axis_index("local")
    mine = node * groups + local // SHARDS
    block = local % SHARDS
    near = block + 1 - 2 * (block % 2)
    far = (block + 2) % SHARDS
    corner = (near + 2) % SHARDS

    def device(expert, which):
        return (expert // groups, (expert % groups) * SHARDS + which)

    return mine, block, near, far, corner, device


def greet(mine, block, near, far, device, experts):
    barrier = pltpu.get_barrier_semaphore()
    targets = [device((mine + r) % experts, block) for r in range(1, experts)]
    targets += [device(mine, near), device(mine, far)]
    for target in targets:
        pl.semaphore_signal(barrier, inc=1, device_id=target, device_id_type=MESH)
    pl.semaphore_wait(barrier, len(targets))


def over_far(r):
    return r % 4 == 0


def rounds(experts, groups):
    same = [r for r in range(experts) if r % groups == 0]
    return same + [r for r in range(experts) if r % groups]


AHEAD = 4
LAG = 2


class Transfer:
    def __init__(self, src, dst, send, recv, slot, target):
        self.copies = [
            pltpu.make_async_remote_copy(
                src_ref=piece,
                dst_ref=landing,
                send_sem=send.at[slot + (k,)],
                recv_sem=recv.at[slot + (k,)],
                device_id=target,
                device_id_type=MESH,
            )
            for k, (piece, landing) in enumerate(zip(src, dst))
        ]

    def start(self):
        for copy in self.copies:
            copy.start()

    def wait_recv(self):
        for copy in self.copies:
            copy.wait_recv()

    def wait_send(self):
        for copy in self.copies:
            copy.wait_send()


def at(refs, *index):
    return [ref.at[index] for ref in refs]


def dispatch_kernel(experts, groups, pieces, *refs):
    bucket, out = refs[:pieces], refs[pieces : 2 * pieces]
    own_sem, a_send, a_recv, b_send, b_recv, c_send, c_recv = refs[2 * pieces :]
    mine, block, near, far, corner, device = place(groups)
    greet(mine, block, near, far, device, experts)

    order = rounds(experts, groups)
    spread, to_near, to_far, relay = {}, {}, {}, {}
    for r in reversed(order[1:]):
        peer = (mine + r) % experts
        spread[r] = Transfer(at(bucket, peer), at(out, block, mine), a_send, a_recv, (r,), device(peer, block))
        spread[r].start()
    own = [
        pltpu.make_async_copy(src, dst, own_sem.at[k])
        for k, (src, dst) in enumerate(zip(at(bucket, mine), at(out, block, mine)))
    ]
    for copy in own:
        copy.start()

    def forward(r):
        source = (mine + experts - r) % experts
        if over_far(r):
            to_near[r].wait_recv()
            moved = at(out, near, source)
            relay[r] = Transfer(moved, moved, c_send, c_recv, (r,), device(mine, far))
        else:
            to_far[r].wait_recv()
            moved = at(out, far, source)
            relay[r] = Transfer(moved, moved, c_send, c_recv, (r,), device(mine, near))
        relay[r].start()

    for step, r in enumerate(order):
        source = (mine + experts - r) % experts
        dst = at(out, block, source)
        if r == 0:
            src = at(bucket, mine)
        else:
            spread[r].wait_recv()
            src = dst
        to_near[r] = Transfer(src, dst, b_send, b_recv, (0, r), device(mine, near))
        to_far[r] = Transfer(src, dst, b_send, b_recv, (1, r), device(mine, far))
        to_near[r].start()
        to_far[r].start()
        if step >= LAG:
            forward(order[step - LAG])
    for r in order[experts - LAG :]:
        forward(r)
    for r in order:
        if over_far(r):
            to_far[r].wait_recv()
        else:
            to_near[r].wait_recv()
        relay[r].wait_recv()
    for r in order:
        if r:
            spread[r].wait_send()
        to_near[r].wait_send()
        to_far[r].wait_send()
        relay[r].wait_send()
    for copy in own:
        copy.wait()


def combine_kernel(experts, groups, pieces, *refs):
    part, ret, held, total, back = [refs[k * pieces : (k + 1) * pieces] for k in range(5)]
    a_send, a_recv, b_send, b_recv, c_send, c_recv = refs[5 * pieces :]
    mine, block, near, far, corner, device = place(groups)
    greet(mine, block, near, far, device, experts)

    def add(dst, *terms):
        for k in range(pieces):
            value = terms[0][k][...].astype(jnp.float32)
            for term in terms[1:]:
                value = value + term[k][...].astype(jnp.float32)
            dst[k][...] = value.astype(dst[k].dtype)

    order = rounds(experts, groups)[::-1]
    relay, to_near, to_far, home = {}, {}, {}, {}

    def open_round(r):
        source = (mine + experts - r) % experts
        target = far if over_far(r) else near
        relay[r] = Transfer(at(part, corner, source), at(held, 2, r), c_send, c_recv, (r,), device(mine, target))
        relay[r].start()
        if over_far(r):
            to_far[r] = Transfer(at(part, far, source), at(held, 1, r), b_send, b_recv, (1, r), device(mine, far))
            to_far[r].start()
        else:
            to_near[r] = Transfer(at(part, near, source), at(held, 0, r), b_send, b_recv, (0, r), device(mine, near))
            to_near[r].start()

    def send_home(r):
        source = (mine + experts - r) % experts
        to_near[r].wait_recv()
        to_far[r].wait_recv()
        terms = at(part, block, source), at(held, 0, r), at(held, 1, r)
        if r == 0:
            add(at(ret, mine), *terms)
        else:
            add(at(back, r), *terms)
            home[r] = Transfer(at(back, r), at(ret, mine), a_send, a_recv, (r,), device(source, block))
            home[r].start()

    for r in order[:AHEAD]:
        open_round(r)
    for step, r in enumerate(order):
        source = (mine + experts - r) % experts
        relay[r].wait_recv()
        if over_far(r):
            add(at(total, r), at(part, near, source), at(held, 2, r))
            to_near[r] = Transfer(at(total, r), at(held, 0, r), b_send, b_recv, (0, r), device(mine, near))
            to_near[r].start()
        else:
            add(at(total, r), at(part, far, source), at(held, 2, r))
            to_far[r] = Transfer(at(total, r), at(held, 1, r), b_send, b_recv, (1, r), device(mine, far))
            to_far[r].start()
        if step + AHEAD < experts:
            open_round(order[step + AHEAD])
        if step >= LAG:
            send_home(order[step - LAG])
    for r in order[experts - LAG :]:
        send_home(r)
    for r in order:
        if r:
            home[r].wait_recv()
            home[r].wait_send()
        relay[r].wait_send()
        to_near[r].wait_send()
        to_far[r].wait_send()


def sems(experts, pieces):
    dma = pltpu.SemaphoreType.DMA
    one, two = dma((experts, pieces)), dma((2, experts, pieces))
    return [one, one, two, two, one, one]


def dispatch(bucket, groups):
    experts, pieces = bucket[0].shape[0], len(bucket)
    return pl.pallas_call(
        functools.partial(dispatch_kernel, experts, groups, pieces),
        out_shape=[jax.ShapeDtypeStruct((SHARDS,) + piece.shape, piece.dtype) for piece in bucket],
        in_specs=[pl.BlockSpec(memory_space=pltpu.VMEM)] * pieces,
        out_specs=[pl.BlockSpec(memory_space=pl.ANY)] * pieces,
        scratch_shapes=[pltpu.SemaphoreType.DMA((pieces,))] + sems(experts, pieces),
        compiler_params=pltpu.CompilerParams(collective_id=0, has_side_effects=True),
        name="dispatch",
    )(*bucket)


def combine(part, groups):
    experts, pieces = part[0].shape[1], len(part)
    blocks = [(piece.shape[1:], piece.dtype) for piece in part]
    return pl.pallas_call(
        functools.partial(combine_kernel, experts, groups, pieces),
        out_shape=[jax.ShapeDtypeStruct(shape, kind) for shape, kind in blocks],
        in_specs=[pl.BlockSpec(memory_space=pltpu.VMEM)] * pieces,
        out_specs=[pl.BlockSpec(memory_space=pltpu.VMEM)] * pieces,
        scratch_shapes=[pltpu.VMEM((3,) + shape, kind) for shape, kind in blocks]
        + [pltpu.VMEM(shape, kind) for shape, kind in blocks] * 2
        + sems(experts, pieces),
        compiler_params=pltpu.CompilerParams(
            collective_id=1, has_side_effects=True, vmem_limit_bytes=60 * 2**20
        ),
        name="combine",
    )(*part)


def dot(left, right):
    return jnp.dot(left, right, preferred_element_type=jnp.float32)


def activate(gate_act, up_act):
    return (jax.nn.silu(gate_act) * up_act).astype(jnp.bfloat16)


def expert_block(rows, w_gate, w_up, w_down):
    hidden = activate(dot(rows, w_gate), dot(rows, w_up))
    return dot(hidden, w_down).astype(jnp.bfloat16)


def folded_block(rows, w_gate, w_up, w_down):
    half = rows.shape[1]

    def project(weight):
        left = dot(rows, weight[:half]).reshape(-1, 2, FOLD, weight.shape[1])
        right = dot(rows, weight[half:]).reshape(-1, 2, FOLD, weight.shape[1])
        return left[:, 0] + right[:, 1]

    hidden = activate(project(w_gate), project(w_up))
    twice = jnp.concatenate([hidden, hidden], axis=1).reshape(rows.shape[0], -1)
    upper = jnp.arange(rows.shape[0])[:, None] % (2 * FOLD) < FOLD
    return jnp.where(upper, dot(twice, w_down[:, :half]), dot(twice, w_down[:, half:])).astype(jnp.bfloat16)


def per_device(tokens, routes, scores, gate_proj, up_proj, down_proj):
    node_count = lax.axis_size("node")
    local_count = lax.axis_size("local")
    token_count, model_width = tokens.shape
    top_count = routes.shape[1]
    groups = local_count // SHARDS
    experts = node_count * groups
    per_expert = max(
        2, token_count * top_count // experts + token_count * top_count // (4 * experts)
    )
    tile = 2 * FOLD
    half = model_width // 2
    full = per_expert // tile * tile
    folds = full > 0 and 0 < per_expert - full <= FOLD
    if not folds:
        full = (per_expert + tile - 1) // tile * tile
    cap = full + FOLD if folds else full
    weights = (SCALE * scores / jnp.sum(scores, axis=1, keepdims=True)).astype(jnp.bfloat16)
    labels = jnp.arange(experts, dtype=jnp.int32)
    matches = routes[:, :, None] == labels[None, None, :]
    routed = jnp.any(matches, axis=1)
    dense_weight = jnp.sum(jnp.where(matches, weights.astype(jnp.float32)[:, :, None], 0.0), axis=1)
    position = jnp.cumsum(routed.astype(jnp.int32), axis=0) - 1
    slot_ids = jnp.arange(cap, dtype=jnp.int32)
    pick = routed.T[:, None, :] & (position.T[:, None, :] == slot_ids[None, :, None])
    slot_pick = pick.astype(jnp.bfloat16)
    slot_weight = jnp.where(pick, dense_weight.T[:, None, :], 0.0).astype(jnp.bfloat16)

    def flat(slots):
        return slots.reshape(-1, slots.shape[-1])

    def halves(slots):
        none = jnp.zeros_like(slots)
        return flat(jnp.concatenate([slots, none], axis=1)), flat(jnp.concatenate([none, slots], axis=1))

    bucket = [dot(flat(slot_pick[:, :full]), tokens).astype(jnp.bfloat16).reshape(experts, full, model_width)]
    if folds:
        upper, lower = halves(slot_pick[:, full:])
        folded = (dot(upper, tokens[:, :half]) + dot(lower, tokens[:, half:])).astype(jnp.bfloat16)
        bucket.append(folded.reshape(experts, tile, half))
    gathered = dispatch(bucket, groups)
    blocks = expert_block, folded_block
    part = [
        blocks[k](flat(piece), gate_proj[0], up_proj[0], down_proj[0]).reshape(piece.shape)
        for k, piece in enumerate(gathered)
    ]
    returned = combine(part, groups)
    combined = dot(flat(slot_weight[:, :full]).T, flat(returned[0]))
    if folds:
        upper, lower = halves(slot_weight[:, full:])
        rows = flat(returned[1])
        combined = combined + jnp.concatenate([dot(upper.T, rows), dot(lower.T, rows)], axis=1)
    return combined.astype(jnp.bfloat16)


def solution(mesh):
    return jax.shard_map(
        per_device,
        mesh=mesh,
        in_specs=(
            P(("node", "local"), None),
            P(("node", "local"), None),
            P(("node", "local"), None),
            P(("node", "local"), None, None),
            P(("node", "local"), None, None),
            P(("node", "local"), None, None),
        ),
        out_specs=P(("node", "local"), None),
        check_vma=False,
    )
```

time: 320 us -> 275 us (0.86)
  Pallas kernels: 282 us -> 235 us
  local copies, waits for them, and re-layouts: 0.25 us -> 5.17 us
  matrix products: 36.4 us -> 32.2 us
    pallas_call x2, Pallas kernels: 282 us -> 235 us  [the longest x1 120 us: dispatch(): pl.pallas_call(functools.partial(dispatch_kernel, experts, groups, pieces...]
    dot_general x5 -> x11, matrix products: 36.4 us -> 27.5 us  [dot(): return jnp.dot(left, right, preferred_element_type=jnp.float32)]
    slice x0 -> x4, matrix products: none -> 4.76 us  [project(): return left[:, 0] + right[:, 1]]
where the time goes in v2:
time: 275 us; the launch traced here: 274 us
  Pallas kernels  235 us (85%)
  matrix products  32.2 us (12%)
  local copies, waits for them, and re-layouts  5.17 us (2%)
    pallas_call x1, Pallas kernels, dispatch(): pl.pallas_call(functools.partial(dispatch_kernel, experts, groups, pieces...  120 us
    pallas_call x1, Pallas kernels, combine(): pl.pallas_call(functools.partial(combine_kernel, experts, groups, pieces)...  115 us
    dot_general x11, matrix products, dot(): return jnp.dot(left, right, preferred_element_type=jnp.float32)  27.5 us

profile of v2, /device:TPU:0, one launch (start us, length us, event | category | flops | bytes accessed | tf_op | source)
XLA Modules:
  0.0 273.8 jit_solution(11665652906222370947)
XLA Ops:
  0.0 0.8 fusion.63
  0.9 0.1 reduce_window_sum.11
  1.1 1.3 fusion.49
  2.4 2.1 fusion.8.refs_1_
  4.4 1.9 convolution_convert_fusion.1
  6.3 119.8 %dispatch.1 = (bf16[4,8,16,7168]{3,2,1,0:T(8,128)(2,1)}, bf16[4,8,8,3584]{3,2,1,0:T(8,128)(2,1)}) custom-call(bf16[8,16,7168]{2,1,0:T(8,128)(2,1)} %bitcast.107, bf16[8,8,3584]{2,1,0:T(8,128)(2,1)} %fusion.8.refs_1_), custom_call_target="tpu_custom_call" | custom-call | tf_op jit(solution)/shard_map/dispatch/pallas_call | solution.py:223
  126.2 2.2 copy.35
  128.4 2.8 %fusion.16 = f32[32,1,4,512]{3,0,2,1:T(8,128)S(1)} fusion(bf16[32,2,4,3584]{3,0,2,1:T(8,128)(2,1)S(1)} %bitcast.108, bf16[1,7168,512]{2,1,0:T(8,128)(2,1)} %param.9), kind=kOutput, calls=%fused_computation.23 | convolution fusion | flops 469762048 | bytes 5767168 | tf_op jit(solution)/shard_map/slice | solution.py:271
  131.2 0.6 slice-done.1
  131.8 0.6 fusion.33
  132.4 0.2 slice-done.3
  132.7 0.6 fusion.12
  133.3 0.7 fusion.45
  134.0 0.8 slice-done.4
  134.9 1.1 slice-done.5
  136.0 1.2 fusion.10
  137.2 2.6 fusion.6
  139.8 4.0 %fusion.4 = f32[512,512]{1,0:T(8,128)S(1)} fusion(bf16[512,7168]{1,0:T(8,128)(2,1)S(1)} %bitcast.127, bf16[1,7168,512]{2,1,0:T(8,128)(2,1)S(1)} %bitcast.118), kind=kOutput, calls=%fused_computation.7 | convolution fusion | flops 3758096384 | bytes 15728640 | tf_op jit(solution)/shard_map/dot_general | solution.py:253
  143.8 4.0 %fusion.27 = bf16[512,512]{1,0:T(8,128)(2,1)S(1)} fusion(bf16[512,7168]{1,0:T(8,128)(2,1)S(1)} %bitcast.128, bf16[1,7168,512]{2,1,0:T(8,128)(2,1)S(1)} %bitcast.120, f32[512,512]{1,0:T(8,128)S(1)} %fusion.4), kind=kOutput, calls=%fused_computation.32 | convolution fusion | flops 3759669248 | bytes 16252928 | tf_op jit(solution)/shard_map/dot_general | solution.py:253
  147.9 6.2 %convolution_convert_fusion = bf16[512,7168]{1,0:T(8,128)(2,1)} fusion(bf16[512,512]{1,0:T(8,128)(2,1)S(1)} %fusion.27, bf16[1,512,7168]{2,1,0:T(8,128)(2,1)S(1)} %bitcast.122), kind=kOutput, calls=%fused_computation | convolution fusion | flops 3761766400 | bytes 15204352 | tf_op jit(solution)/shard_map/dot_general | solution.py:253
  154.1 115.4 %combine.1 = (bf16[8,16,7168]{2,1,0:T(8,128)(2,1)}, bf16[8,8,3584]{2,1,0:T(8,128)(2,1)}) custom-call(bf16[4,8,16,7168]{3,2,1,0:T(8,128)(2,1)} %bitcast.106, bf16[4,8,8,3584]{3,2,1,0:T(8,128)(2,1)} %bitcast.112), custom_call_target="tpu_custom_call" | custom-call | tf_op jit(solution)/shard_map/combine/pallas_call | solution.py:237
  269.6 1.5 convolution_bitcast_fusion.2
  271.0 1.4 convolution_bitcast_fusion.1
  272.4 1.4 fusion.1
  (38 shorter events, 0.4 us)
Async XLA Ops:
  0.0 4.4 %copy-start = (bf16[64,7168]{1,0:T(8,128)(2,1)S(1)}, bf16[64,7168]{1,0:T(8,128)(2,1)}, u32[]{:S(2)}) copy-start(bf16[64,7168]{1,0:T(8,128)(2,1)} %param.6) | copy-start | bytes 2752516
  6.3 124.9 %slice-start = ((s8[7340032]{0:T(1024)(128)(4,1)}), s8[3145728]{0:T(1024)(128)(4,1)S(1)}, s32[]{:S(2)}) async-start(s8[7340032]{0:T(1024)(128)(4,1)} %bitcast.117), calls=%async_computation | async-start | bytes 6291456
  126.1 6.3 %slice-start.2 = ((s8[7340032]{0:T(1024)(128)(4,1)}), s8[4194304]{0:T(1024)(128)(4,1)S(1)}, s32[]{:S(2)}) async-start(s8[7340032]{0:T(1024)(128)(4,1)} %bitcast.119), calls=%async_computation.2 | async-start | bytes 8388608
  128.3 3.4 %slice-start.1 = ((s8[7340032]{0:T(1024)(128)(4,1)}), s8[4194304]{0:T(1024)(128)(4,1)S(1)}, s32[]{:S(2)}) async-start(s8[7340032]{0:T(1024)(128)(4,1)} %bitcast.117), calls=%async_computation.1 | async-start | bytes 8388608
  128.4 4.3 %slice-start.3 = ((s8[7340032]{0:T(1024)(128)(4,1)}), s8[3145728]{0:T(1024)(128)(4,1)S(1)}, s32[]{:S(2)}) async-start(s8[7340032]{0:T(1024)(128)(4,1)} %bitcast.119), calls=%async_computation.3 | async-start | bytes 6291456
  132.7 2.2 slice-start.4
  133.3 2.7 slice-start.5
  136.0 3.8 %slice-start.6 = ((s8[7340032]{0:T(1024)(128)(4,1)}), s8[4194304]{0:T(1024)(128)(4,1)S(1)}, s32[]{:S(2)}) async-start(s8[7340032]{0:T(1024)(128)(4,1)} %bitcast.125), calls=%async_computation.6 | async-start | bytes 8388608
  137.2 2.6 slice-start.7
  154.1 115.4 %copy-start.2 = (f32[64,2]{0,1:T(2,128)S(1)}, f32[64,2]{0,1:T(2,128)}, u32[]{:S(2)}) copy-start(f32[64,2]{0,1:T(2,128)} %param.8) | copy-start | bytes 1540
  154.1 115.4 %copy-start.3 = (s32[64,2]{0,1:T(2,128)S(1)}, s32[64,2]{0,1:T(2,128)}, u32[]{:S(2)}) copy-start(s32[64,2]{0,1:T(2,128)} %param.7) | copy-start | bytes 1540
  269.4 2.9 %copy-start.1 = (bf16[8,16,7168]{2,1,0:T(8,128)(2,1)S(1)}, bf16[8,16,7168]{2,1,0:T(8,128)(2,1)}, u32[]{:S(2)}) copy-start(bf16[8,16,7168]{2,1,0:T(8,128)(2,1)} %get-tuple-element.11) | copy-start | bytes 5505028

commit v3 on v2

--- a/solution.py
+++ b/solution.py
@@ -37,8 +37,8 @@
     pl.semaphore_wait(barrier, len(targets))
 
 
-def over_far(r):
-    return r % 4 == 0
+def over_far(r, every):
+    return every > 0 and r % every == 0
 
 
 def rounds(experts, groups):
@@ -46,6 +46,8 @@
     return same + [r for r in range(experts) if r % groups]
 
 
+DISPATCH_FAR = 4
+COMBINE_FAR = 0
 AHEAD = 4
 LAG = 2
 
@@ -102,7 +104,7 @@
 
     def forward(r):
         source = (mine + experts - r) % experts
-        if over_far(r):
+        if over_far(r, DISPATCH_FAR):
             to_near[r].wait_recv()
             moved = at(out, near, source)
             relay[r] = Transfer(moved, moved, c_send, c_recv, (r,), device(mine, far))
@@ -129,7 +131,7 @@
     for r in order[experts - LAG :]:
         forward(r)
     for r in order:
-        if over_far(r):
+        if over_far(r, DISPATCH_FAR):
             to_far[r].wait_recv()
         else:
             to_near[r].wait_recv()
@@ -162,10 +164,10 @@
 
     def open_round(r):
         source = (mine + experts - r) % experts
-        target = far if over_far(r) else near
+        target = far if over_far(r, COMBINE_FAR) else near
         relay[r] = Transfer(at(part, corner, source), at(held, 2, r), c_send, c_recv, (r,), device(mine, target))
         relay[r].start()
-        if over_far(r):
+        if over_far(r, COMBINE_FAR):
             to_far[r] = Transfer(at(part, far, source), at(held, 1, r), b_send, b_recv, (1, r), device(mine, far))
             to_far[r].start()
         else:
@@ -189,7 +191,7 @@
     for step, r in enumerate(order):
         source = (mine + experts - r) % experts
         relay[r].wait_recv()
-        if over_far(r):
+        if over_far(r, COMBINE_FAR):
             add(at(total, r), at(part, near, source), at(held, 2, r))
             to_near[r] = Transfer(at(total, r), at(held, 0, r), b_send, b_recv, (0, r), device(mine, near))
             to_near[r].start()

time: 275 us -> 271 us (0.985)
  Pallas kernels: 235 us -> 230 us
    pallas_call x1, Pallas kernels: 115 us -> 111 us  [combine(): pl.pallas_call(functools.partial(combine_kernel, experts, groups, pieces)...]
where the time goes in v3:
time: 271 us; the launch traced here: 269 us
  Pallas kernels  230 us (85%)
  matrix products  32.2 us (12%)
  local copies, waits for them, and re-layouts  5.17 us (2%)
    pallas_call x1, Pallas kernels, dispatch(): pl.pallas_call(functools.partial(dispatch_kernel, experts, groups, pieces...  120 us
    pallas_call x1, Pallas kernels, combine(): pl.pallas_call(functools.partial(combine_kernel, experts, groups, pieces)...  111 us
    dot_general x11, matrix products, dot(): return jnp.dot(left, right, preferred_element_type=jnp.float32)  27.5 us

profile of v3, /device:TPU:0, one launch (start us, length us, event | category | flops | bytes accessed | tf_op | source)
XLA Modules:
  0.0 269.0 jit_solution(290016330168002320)
XLA Ops:
  0.0 0.8 fusion.63
  0.9 0.1 reduce_window_sum.11
  1.1 1.3 fusion.49
  2.4 2.1 fusion.8.refs_1_
  4.4 1.9 convolution_convert_fusion.1
  6.3 119.8 %dispatch.1 = (bf16[4,8,16,7168]{3,2,1,0:T(8,128)(2,1)}, bf16[4,8,8,3584]{3,2,1,0:T(8,128)(2,1)}) custom-call(bf16[8,16,7168]{2,1,0:T(8,128)(2,1)} %bitcast.107, bf16[8,8,3584]{2,1,0:T(8,128)(2,1)} %fusion.8.refs_1_), custom_call_target="tpu_custom_call" | custom-call | tf_op jit(solution)/shard_map/dispatch/pallas_call | solution.py:225
  126.2 2.2 copy.35
  128.4 2.8 %fusion.16 = f32[32,1,4,512]{3,0,2,1:T(8,128)S(1)} fusion(bf16[32,2,4,3584]{3,0,2,1:T(8,128)(2,1)S(1)} %bitcast.108, bf16[1,7168,512]{2,1,0:T(8,128)(2,1)} %param.9), kind=kOutput, calls=%fused_computation.23 | convolution fusion | flops 469762048 | bytes 5767168 | tf_op jit(solution)/shard_map/slice | solution.py:273
  131.2 0.6 slice-done.1
  131.8 0.6 fusion.33
  132.4 0.2 slice-done.3
  132.7 0.6 fusion.12
  133.3 0.7 fusion.45
  134.0 0.8 slice-done.4
  134.9 1.1 slice-done.5
  136.0 1.2 fusion.10
  137.2 2.6 fusion.6
  139.8 4.0 %fusion.4 = f32[512,512]{1,0:T(8,128)S(1)} fusion(bf16[512,7168]{1,0:T(8,128)(2,1)S(1)} %bitcast.127, bf16[1,7168,512]{2,1,0:T(8,128)(2,1)S(1)} %bitcast.118), kind=kOutput, calls=%fused_computation.7 | convolution fusion | flops 3758096384 | bytes 15728640 | tf_op jit(solution)/shard_map/dot_general | solution.py:255
  143.8 4.0 %fusion.27 = bf16[512,512]{1,0:T(8,128)(2,1)S(1)} fusion(bf16[512,7168]{1,0:T(8,128)(2,1)S(1)} %bitcast.128, bf16[1,7168,512]{2,1,0:T(8,128)(2,1)S(1)} %bitcast.120, f32[512,512]{1,0:T(8,128)S(1)} %fusion.4), kind=kOutput, calls=%fused_computation.32 | convolution fusion | flops 3759669248 | bytes 16252928 | tf_op jit(solution)/shard_map/dot_general | solution.py:255
  147.9 6.2 %convolution_convert_fusion = bf16[512,7168]{1,0:T(8,128)(2,1)} fusion(bf16[512,512]{1,0:T(8,128)(2,1)S(1)} %fusion.27, bf16[1,512,7168]{2,1,0:T(8,128)(2,1)S(1)} %bitcast.122), kind=kOutput, calls=%fused_computation | convolution fusion | flops 3761766400 | bytes 15204352 | tf_op jit(solution)/shard_map/dot_general | solution.py:255
  154.1 110.6 %combine.1 = (bf16[8,16,7168]{2,1,0:T(8,128)(2,1)}, bf16[8,8,3584]{2,1,0:T(8,128)(2,1)}) custom-call(bf16[4,8,16,7168]{3,2,1,0:T(8,128)(2,1)} %bitcast.106, bf16[4,8,8,3584]{3,2,1,0:T(8,128)(2,1)} %bitcast.112), custom_call_target="tpu_custom_call" | custom-call | tf_op jit(solution)/shard_map/combine/pallas_call | solution.py:239
  264.8 1.5 convolution_bitcast_fusion.2
  266.2 1.4 convolution_bitcast_fusion.1
  267.6 1.4 fusion.1
  (38 shorter events, 0.4 us)
Async XLA Ops:
  0.0 4.4 %copy-start = (bf16[64,7168]{1,0:T(8,128)(2,1)S(1)}, bf16[64,7168]{1,0:T(8,128)(2,1)}, u32[]{:S(2)}) copy-start(bf16[64,7168]{1,0:T(8,128)(2,1)} %param.6) | copy-start | bytes 2752516
  6.3 124.9 %slice-start = ((s8[7340032]{0:T(1024)(128)(4,1)}), s8[3145728]{0:T(1024)(128)(4,1)S(1)}, s32[]{:S(2)}) async-start(s8[7340032]{0:T(1024)(128)(4,1)} %bitcast.117), calls=%async_computation | async-start | bytes 6291456
  126.1 6.3 %slice-start.2 = ((s8[7340032]{0:T(1024)(128)(4,1)}), s8[4194304]{0:T(1024)(128)(4,1)S(1)}, s32[]{:S(2)}) async-start(s8[7340032]{0:T(1024)(128)(4,1)} %bitcast.119), calls=%async_computation.2 | async-start | bytes 8388608
  128.3 3.4 %slice-start.1 = ((s8[7340032]{0:T(1024)(128)(4,1)}), s8[4194304]{0:T(1024)(128)(4,1)S(1)}, s32[]{:S(2)}) async-start(s8[7340032]{0:T(1024)(128)(4,1)} %bitcast.117), calls=%async_computation.1 | async-start | bytes 8388608
  128.4 4.3 %slice-start.3 = ((s8[7340032]{0:T(1024)(128)(4,1)}), s8[3145728]{0:T(1024)(128)(4,1)S(1)}, s32[]{:S(2)}) async-start(s8[7340032]{0:T(1024)(128)(4,1)} %bitcast.119), calls=%async_computation.3 | async-start | bytes 6291456
  132.7 2.2 slice-start.4
  133.3 2.7 slice-start.5
  136.0 3.8 %slice-start.6 = ((s8[7340032]{0:T(1024)(128)(4,1)}), s8[4194304]{0:T(1024)(128)(4,1)S(1)}, s32[]{:S(2)}) async-start(s8[7340032]{0:T(1024)(128)(4,1)} %bitcast.125), calls=%async_computation.6 | async-start | bytes 8388608
  137.2 2.6 slice-start.7
  154.1 110.6 %copy-start.2 = (f32[64,2]{0,1:T(2,128)S(1)}, f32[64,2]{0,1:T(2,128)}, u32[]{:S(2)}) copy-start(f32[64,2]{0,1:T(2,128)} %param.8) | copy-start | bytes 1540
  154.1 110.6 %copy-start.3 = (s32[64,2]{0,1:T(2,128)S(1)}, s32[64,2]{0,1:T(2,128)}, u32[]{:S(2)}) copy-start(s32[64,2]{0,1:T(2,128)} %param.7) | copy-start | bytes 1540
  264.6 2.9 %copy-start.1 = (bf16[8,16,7168]{2,1,0:T(8,128)(2,1)S(1)}, bf16[8,16,7168]{2,1,0:T(8,128)(2,1)}, u32[]{:S(2)}) copy-start(bf16[8,16,7168]{2,1,0:T(8,128)(2,1)} %get-tuple-element.11) | copy-start | bytes 5505028
